TPU v7x, 32 devices: a whole 2x2x4 slice. The times are simulated.
32 devices in a mesh: expert: 4 (over y, core), shard: 8 (over z, x).
Axes of the slice: x: 2, y: 2, z: 4, core: 2. Of those that a mesh axis runs over, the one named last changes fastest.
Arguments:
- w_gate: float32 [128, 2048, 768], P('expert', 'shard'), may hold values from -0.1875 to 0.1875
- w_up: float32 [128, 2048, 768], P('expert', 'shard'), may hold values from -0.1875 to 0.1875
- router_weight: float32 [2048, 128], P('shard', 'expert'), may hold values from -0.125 to 0.125
- router_gain: float32 [2048], P('shard'), may hold values from 0.25 to 1.75
Outputs:
- serve_gate: bfloat16 [128, 2048, 768], P('expert', None, 'shard')
- serve_up: bfloat16 [128, 2048, 768], P('expert', None, 'shard')
- scale_gate: float32 [128, 768], P('expert', 'shard')
- scale_up: float32 [128, 768], P('expert', 'shard')
- serve_router: bfloat16 [2048, 128], replicated
All inputs are finite; a program needn't handle non-finite values. Where the computation divides by a largest or mean magnitude, that divisor is 1e-20 or more.
Results may differ from a plain program's by a relative error of at most 0.001.
Values may be sent and summed in bfloat16 or wider, within the bound.
A program may use at most 192 MiB of HBM per device.

v0:
```python
import jax
import jax.numpy as jnp
from jax import lax
from jax.sharding import PartitionSpec as P


def body(w_gate, w_up, router_weight, router_gain):
    scale_gate, scale_up = lax.pmax(
        (jnp.max(jnp.abs(w_gate), axis=1), jnp.max(jnp.abs(w_up), axis=1)), "shard"
    )
    narrow_gate, narrow_up = (
        (w_gate / jnp.expand_dims(scale_gate, 1)).astype(jnp.bfloat16),
        (w_up / jnp.expand_dims(scale_up, 1)).astype(jnp.bfloat16),
    )
    serve_gate, serve_up = (
        lax.all_to_all(narrow_gate, "shard", split_axis=2, concat_axis=1, tiled=True),
        lax.all_to_all(narrow_up, "shard", split_axis=2, concat_axis=1, tiled=True),
    )
    scale_gate = lax.dynamic_slice_in_dim(
        scale_gate, lax.axis_index("shard") * serve_gate.shape[2], serve_gate.shape[2], axis=1
    )
    scale_up = lax.dynamic_slice_in_dim(
        scale_up, lax.axis_index("shard") * serve_up.shape[2], serve_up.shape[2], axis=1
    )
    part_router = (router_weight * router_gain[:, None]).astype(jnp.bfloat16)
    row_router = lax.all_gather(part_router, "shard", axis=0, tiled=True)
    serve_router = lax.all_gather(row_router, "expert", axis=1, tiled=True)
    return (serve_gate, serve_up, scale_gate, scale_up, serve_router)


def solution(mesh):
    return jax.shard_map(
        body,
        mesh=mesh,
        in_specs=(
            P("expert", "shard", None),
            P("expert", "shard", None),
            P("shard", "expert"),
            P("shard"),
        ),
        out_specs=(
            P("expert", None, "shard"),
            P("expert", None, "shard"),
            P("expert", "shard"),
            P("expert", "shard"),
            P(),
        ),
        check_vma=False,
    )
```

profile of v0, /device:TPU:0, one launch (start us, length us, event | category | flops | bytes accessed | tf_op | source)
XLA Modules:
  0.0 771.9 jit_solution(16742101143083610115)
XLA Ops:
  7.2 0.0 all-reduce.3.cloned.1.call-start
  7.2 0.0 copy-start
  7.2 10.2 %abs_reduce_fusion = f32[32,768]{1,0:T(8,128)} fusion(f32[32,256,768]{2,1,0:T(8,128)} %param.5), kind=kLoop, calls=%fused_computation.1 | loop fusion | flops 12558336 | bytes 25264128 | tf_op jit(solution)/shard_map/reduce_max | solution.py:9
  17.4 5.3 copy-done
  22.7 3.0 abs_reduce_fusion.1
  25.7 0.0 all-reduce.3.cloned.1.call-update
  25.7 25.1 %copy.21 = f32[32,256,768]{1,0,2:T(8,128)} copy(f32[32,256,768]{2,1,0:T(8,128)} %param.4) | data formatting | bytes 50331648 | tf_op args[0]
  50.8 48.8 %all-reduce.3.cloned.1.call-done = (f32[32,768]{1,0:T(8,128)}, f32[32,768]{1,0:T(8,128)}) async-done(((f32[32,768]{1,0:T(8,128)}, f32[32,768]{1,0:T(8,128)}), (f32[32,768]{1,0:T(8,128)}, f32[32,768]{1,0:T(8,128)})) %all-reduce.3.cloned.1.call-update) | async-done | bytes 196624 | tf_op jit(solution)/shard_map/pmax | solution.py:8
  99.6 1.1 copy.20
  100.7 14.1 %divide_convert_fusion.1 = bf16[32,256,768]{1,0,2:T(8,128)(2,1)} fusion(f32[32,256,768]{1,0,2:T(8,128)} %copy.21, f32[32,768]{0,1:T(8,128)S(1)} %copy.20), kind=kLoop, calls=%fused_computation.2 | loop fusion | flops 12582912 | bytes 37847040 | tf_op jit(solution)/shard_map/convert_element_type | solution.py:12
  114.8 5.4 all-to-all-start
  120.2 0.0 copy-start.1
  120.2 25.1 %copy.25 = f32[32,256,768]{1,0,2:T(8,128)} copy(f32[32,256,768]{2,1,0:T(8,128)} %param.5) | data formatting | bytes 50331648 | tf_op args[1]
  145.3 0.0 copy-done.1
  145.3 0.2 copy.24
  145.5 0.0 copy-start.2
  145.5 0.0 copy-start.3
  145.5 14.1 %divide_convert_fusion = bf16[32,256,768]{1,0,2:T(8,128)(2,1)} fusion(f32[32,256,768]{1,0,2:T(8,128)} %copy.25, f32[32,768]{0,1:T(8,128)S(1)} %copy.24), kind=kLoop, calls=%fused_computation | loop fusion | flops 12582912 | bytes 37847040 | tf_op jit(solution)/shard_map/convert_element_type | solution.py:13
  159.6 231.8 %all-to-all-done = bf16[32,256,768]{1,0,2:T(8,128)(2,1)} async-done(((bf16[32,256,768]{1,0,2:T(8,128)(2,1)}), bf16[32,256,768]{1,0,2:T(8,128)(2,1)}, u32[]{:S(2)}, u32[]{:S(2)}) %all-to-all-start) | async-done | bytes 12582944 | tf_op jit(solution)/shard_map/all_to_all | solution.py:16
  391.4 5.3 all-to-all-start.1
  396.7 0.0 copy-done.2
  396.7 0.0 copy-done.3
  396.8 291.6 %all_gather.6 = bf16[2048,32]{0,1:T(8,128)(2,1)S(1)} all-gather(bf16[256,32]{0,1:T(8,128)(2,1)S(1)} %multiply_convert_fusion), channel_id=1, replica_groups=mesh['expert'=4,'shard'=8] {'shard'}, dimensions={0}, use_global_device_ids=true | all-gather | bytes 147456 | tf_op jit(solution)/shard_map/all_gather | solution.py:26
  688.4 7.1 all_gather.7
  695.5 1.0 copy.28
  696.5 1.4 constant_dynamic-slice_fusion
  698.0 14.1 %copy.23 = bf16[32,8,256,96]{2,1,3,0:T(8,128)(2,1)} copy(bf16[32,8,256,96]{2,0,3,1:T(8,128)(2,1)} %bitcast.2) | data formatting | bytes 25165824 | tf_op jit(solution)/shard_map/all_to_all | solution.py:16
  712.0 19.5 %all_to_all.29 = bf16[32,2048,96]{1,2,0:T(8,128)(2,1)} reshape(bf16[32,8,256,96]{2,1,3,0:T(8,128)(2,1)} %copy.23) | data formatting | bytes 25165824 | tf_op jit(solution)/shard_map/all_to_all | solution.py:16
  731.5 0.0 all-to-all-done.1
  731.5 14.1 %copy.27 = bf16[32,8,256,96]{2,1,3,0:T(8,128)(2,1)} copy(bf16[32,8,256,96]{2,0,3,1:T(8,128)(2,1)} %bitcast.5) | data formatting | bytes 25165824 | tf_op jit(solution)/shard_map/all_to_all | solution.py:17
  745.6 19.5 %all_to_all.33 = bf16[32,2048,96]{1,2,0:T(8,128)(2,1)} reshape(bf16[32,8,256,96]{2,1,3,0:T(8,128)(2,1)} %copy.27) | data formatting | bytes 25165824 | tf_op jit(solution)/shard_map/all_to_all | solution.py:17
  (1 shorter events, 0.0 us)
Async XLA Ops:
  7.2 92.4 %all-reduce.3.cloned.1.call-start = ((), (), s32[]{:S(2)}) async-start(), calls=%async_computation.2 | async-start | bytes 393216 | tf_op jit(solution)/shard_map/pmax | solution.py:8
  7.2 15.5 %copy-start = (f32[32,256,768]{2,1,0:T(8,128)S(1)}, f32[32,256,768]{2,1,0:T(8,128)}, u32[]{:S(2)}) copy-start(f32[32,256,768]{2,1,0:T(8,128)} %param.4) | copy-start | bytes 75497472
  114.8 276.6 %all-to-all-start = ((bf16[32,256,768]{1,0,2:T(8,128)(2,1)}), bf16[32,256,768]{1,0,2:T(8,128)(2,1)}, u32[]{:S(2)}, u32[]{:S(2)}) async-start(bf16[32,256,768]{1,0,2:T(8,128)(2,1)} %divide_convert_fusion.1), calls=%async_computation | async-start | bytes 25165824 | tf_op jit(solution)/shard_map/all_to_all | solution.py:16
  120.2 25.1 %copy-start.1 = (f32[32,768]{1,0:T(8,128)S(1)}, f32[32,768]{1,0:T(8,128)}, u32[]{:S(2)}) copy-start(f32[32,768]{1,0:T(8,128)} %get-tuple-element.11) | copy-start | bytes 294916
  145.5 251.3 %copy-start.2 = (f32[256,32]{0,1:T(8,128)S(1)}, f32[256,32]{0,1:T(8,128)}, u32[]{:S(2)}) copy-start(f32[256,32]{0,1:T(8,128)} %param.6) | copy-start | bytes 98308
  145.5 251.3 %copy-start.3 = (f32[256]{0:T(256)S(1)}, f32[256]{0:T(256)}, u32[]{:S(2)}) copy-start(f32[256]{0:T(256)} %param.7) | copy-start | bytes 3076
  391.4 340.1 %all-to-all-start.1 = ((bf16[32,256,768]{1,0,2:T(8,128)(2,1)}), bf16[32,256,768]{1,0,2:T(8,128)(2,1)}, u32[]{:S(2)}, u32[]{:S(2)}) async-start(bf16[32,256,768]{1,0,2:T(8,128)(2,1)} %divide_convert_fusion), calls=%async_computation.1 | async-start | bytes 25165824 | tf_op jit(solution)/shard_map/all_to_all | solution.py:17
Sparse Core Ops, SparseCore 0:
  25.9 73.6 all-reduce.2
where the time goes:
time: 774 us; the launch traced here: 772 us
  blocking collectives  299 us (39%)
  waiting for transfers between devices  281 us (36%)
  local copies, waits for them, and re-layouts  126 us (16%)
  other arithmetic  41.5 us (5%)
  between operations  14.1 us (2%)
  starting transfers between devices  10.8 us (1%)
    all_gather x1, blocking collectives, body(): row_router = lax.all_gather(part_router, 'shard', axis=0, tiled=True)  292 us
    all_to_all x1, waiting for transfers between devices, body(): lax.all_to_all(narrow_gate, 'shard', split_axis=2, concat_axis=1, tiled=T...  232 us
    unnamed x11, local copies, waits for them, and re-layouts  56.4 us
    pmax x1, waiting for transfers between devices, body(): lax.pmax((jnp.max(jnp.abs(w_gate), axis=1), jnp.max(jnp.abs(w_up), axis=1...  48.8 us
    all_to_all x2, local copies, waits for them, and re-layouts, body(): lax.all_to_all(narrow_up, 'shard', split_axis=2, concat_axis=1, tiled=True)  33.6 us
    all_to_all x2, local copies, waits for them, and re-layouts, body(): lax.all_to_all(narrow_gate, 'shard', split_axis=2, concat_axis=1, tiled=T...  33.5 us
  transfers between devices with their start and end apart: 3, of which 2 were waited for; matrix products, arithmetic and copies ran while one was open for 10% of the time, Pallas kernels for 0%

commit v1 on v0

--- a/solution.py
+++ b/solution.py
@@ -1,10 +1,219 @@
+import functools
+import math
+
 import jax
 import jax.numpy as jnp
 from jax import lax
+from jax.experimental import pallas as pl
+from jax.experimental.pallas import tpu as pltpu
 from jax.sharding import PartitionSpec as P
 
-
-def body(w_gate, w_up, router_weight, router_gain):
+MESH = pl.DeviceIdType.MESH
+SLOTS = 4
+LANES = 128
+
+
+def kernel(
+    n, ne, chunk,
+    gate, up, router, gain,
+    out_gate, out_up, out_scale, out_router,
+    ring, send, lmax, rs, gm, rbuf,
+    load_sem, own_sem, send_sem, recv_sem,
+    rs_send, rs_recv, ag_send, ag_recv,
+    r1_send, r1_recv, r2_send, r2_recv,
+):
+    me = lax.axis_index("shard")
+    my_e = lax.axis_index("expert")
+    experts, rows, cols = gate.shape
+    part = cols // n
+    share = experts // n
+    chunks = experts // chunk
+    outs = (out_gate, out_up)
+
+    offsets = sorted(range(1, n), key=lambda r: (abs(r - n // 2), r))
+
+    def ahead(r):
+        return lax.rem(me + r, n)
+
+    def behind(r):
+        return lax.rem(me + (n - r), n)
+
+    def load(array, index, slot):
+        return pltpu.make_async_copy(
+            array.at[pl.ds(index * chunk, chunk)], ring.at[slot], load_sem.at[slot]
+        )
+
+    def start_load(k):
+        slot, index, which = k % SLOTS, k % chunks, (k // chunks) % 2
+
+        @pl.when((k < 4 * chunks) & (which == 0))
+        def _():
+            load(gate, index, slot).start()
+
+        @pl.when((k < 4 * chunks) & (which == 1))
+        def _():
+            load(up, index, slot).start()
+
+    for k in range(SLOTS):
+        load((gate, up)[(k // chunks) % 2], k % chunks, k).start()
+
+    barrier = pltpu.get_barrier_semaphore()
+    for r in range(1, n):
+        pl.semaphore_signal(barrier, inc=1, device_id={"shard": ahead(r)}, device_id_type=MESH)
+    for r in range(1, ne):
+        pl.semaphore_signal(
+            barrier, inc=1, device_id={"expert": lax.rem(my_e + r, ne)}, device_id_type=MESH
+        )
+
+    rbuf[my_e, me] = (router[...] * gain[...]).astype(jnp.bfloat16)
+
+    pl.semaphore_wait(barrier, n + ne - 2)
+
+    def router_row(r, slot):
+        return pltpu.make_async_remote_copy(
+            src_ref=rbuf.at[my_e, me], dst_ref=rbuf.at[my_e, slot],
+            send_sem=r1_send.at[r], recv_sem=r1_recv.at[r],
+            device_id={"shard": ahead(r)}, device_id_type=MESH,
+        )
+
+    def router_col(r, slot):
+        return pltpu.make_async_remote_copy(
+            src_ref=rbuf.at[my_e], dst_ref=rbuf.at[slot],
+            send_sem=r2_send.at[r], recv_sem=r2_recv.at[r],
+            device_id={"expert": lax.rem(my_e + r, ne)}, device_id_type=MESH,
+        )
+
+    def spread(a, r, slot):
+        return pltpu.make_async_remote_copy(
+            src_ref=lmax.at[a, pl.ds(ahead(r) * share, share)], dst_ref=rs.at[a, slot],
+            send_sem=rs_send.at[a, r], recv_sem=rs_recv.at[a, r],
+            device_id={"shard": ahead(r)}, device_id_type=MESH,
+        )
+
+    def collect(a, r, slot):
+        return pltpu.make_async_remote_copy(
+            src_ref=gm.at[a, pl.ds(me * share, share)],
+            dst_ref=gm.at[a, pl.ds(slot * share, share)],
+            send_sem=ag_send.at[a, r], recv_sem=ag_recv.at[a, r],
+            device_id={"shard": ahead(r)}, device_id_type=MESH,
+        )
+
+    def column(slot):
+        return pl.ds(pl.multiple_of(slot * rows, LANES), rows)
+
+    def peer_rows(slot):
+        return pl.ds(pl.multiple_of(slot * part, 16), part)
+
+    def piece(a, r, slot, first, count):
+        return pltpu.make_async_remote_copy(
+            src_ref=send.at[a, pl.ds(first, count), peer_rows(ahead(r))],
+            dst_ref=outs[a].at[pl.ds(first, count), :, column(slot)],
+            send_sem=send_sem.at[a, r], recv_sem=recv_sem.at[a, r],
+            device_id={"shard": ahead(r)}, device_id_type=MESH,
+        )
+
+    def own(a, first, count):
+        return pltpu.make_async_copy(
+            send.at[a, pl.ds(first, count), peer_rows(me)],
+            outs[a].at[pl.ds(first, count), :, column(me)],
+            own_sem.at[a],
+        )
+
+    def maxima(a):
+        @pl.loop(0, chunks)
+        def _(c):
+            k = a * chunks + c
+            slot = k % SLOTS
+            load(gate, 0, slot).wait()
+
+            @pl.loop(0, chunk)
+            def _(i):
+                lmax[a, c * chunk + i] = jnp.max(jnp.abs(ring[slot, i]), axis=0, keepdims=True)
+
+            start_load(k + SLOTS)
+
+    def reduce(a):
+        largest = lmax[a, pl.ds(me * share, share)]
+        for r in offsets:
+            spread(a, r, behind(r)).wait_recv()
+            largest = jnp.maximum(largest, rs[a, behind(r)])
+        gm[a, pl.ds(me * share, share)] = largest
+
+    def ship(a, first):
+        for r in offsets:
+            piece(a, r, me, first, chunk).start()
+        own(a, first, chunk).start()
+
+    def quotients(a):
+        @pl.loop(0, chunks)
+        def _(c):
+            k = (2 + a) * chunks + c
+            slot = k % SLOTS
+            load(gate, 0, slot).wait()
+
+            @pl.loop(0, chunk)
+            def _(i):
+                e = c * chunk + i
+                inverse = 1.0 / gm[a, e]
+                for j in range(0, cols, LANES):
+                    block = ring[slot, i, :, j:j + LANES] * inverse[:, j:j + LANES]
+                    send[a, e, j:j + LANES, :] = block.T.astype(jnp.bfloat16)
+
+            start_load(k + SLOTS)
+
+            @pl.when(c > 0)
+            def _():
+                ship(a, (c - 1) * chunk)
+
+        ship(a, (chunks - 1) * chunk)
+
+    for r in offsets:
+        router_row(r, me).start()
+    maxima(0)
+    for r in offsets:
+        spread(0, r, me).start()
+    maxima(1)
+    for r in offsets:
+        spread(1, r, me).start()
+    reduce(0)
+    for r in offsets:
+        collect(0, r, me).start()
+    reduce(1)
+    for r in offsets:
+        collect(1, r, me).start()
+    for r in offsets:
+        collect(0, r, behind(r)).wait_recv()
+    quotients(0)
+    for r in offsets:
+        collect(1, r, behind(r)).wait_recv()
+    quotients(1)
+
+    for r in offsets:
+        router_row(r, behind(r)).wait_recv()
+    for r in range(1, ne):
+        router_col(r, my_e).start()
+    out_scale[...] = gm[...]
+    for r in range(1, ne):
+        router_col(r, lax.rem(my_e + (ne - r), ne)).wait_recv()
+    for s in range(n):
+        block = rbuf[:, s].astype(jnp.float32).reshape(ne * rbuf.shape[2], rows)
+        out_router[s * rows:(s + 1) * rows, :] = block.T.astype(jnp.bfloat16)
+
+    for r in offsets:
+        router_row(r, me).wait_send()
+        for a in range(2):
+            spread(a, r, me).wait_send()
+            collect(a, r, me).wait_send()
+    for r in range(1, ne):
+        router_col(r, my_e).wait_send()
+    for a in range(2):
+        own(a, 0, experts).wait()
+        for r in offsets:
+            piece(a, r, me, 0, experts).wait_send()
+            piece(a, r, behind(r), 0, experts).wait_recv()
+
+
+def plain_body(w_gate, w_up, router_weight, router_gain):
     scale_gate, scale_up = lax.pmax(
         (jnp.max(jnp.abs(w_gate), axis=1), jnp.max(jnp.abs(w_up), axis=1)), "shard"
     )
@@ -28,9 +237,61 @@
     return (serve_gate, serve_up, scale_gate, scale_up, serve_router)
 
 
+def body(n, ne, w_gate, w_up, router_weight, router_gain):
+    experts, rows, cols = w_gate.shape
+    if rows % LANES or cols % LANES or (cols // n) % 16 or experts % n:
+        return plain_body(w_gate, w_up, router_weight, router_gain)
+    part, share = cols // n, experts // n
+    chunk = math.gcd(experts, 4)
+    serve = jax.ShapeDtypeStruct((experts, part, n * rows), jnp.bfloat16)
+    dma = pltpu.SemaphoreType.DMA
+    anywhere = pl.BlockSpec(memory_space=pl.ANY)
+    local = pl.BlockSpec(memory_space=pltpu.VMEM)
+    gate, up, scale, router = pl.pallas_call(
+        functools.partial(kernel, n, ne, chunk),
+        out_shape=(
+            serve,
+            serve,
+            jax.ShapeDtypeStruct((2, experts, 1, cols), jnp.float32),
+            jax.ShapeDtypeStruct((n * rows, ne * router_weight.shape[1]), jnp.bfloat16),
+        ),
+        in_specs=[anywhere, anywhere, local, local],
+        out_specs=(anywhere, anywhere, local, local),
+        scratch_shapes=[
+            pltpu.VMEM((SLOTS, chunk, rows, cols), jnp.float32),
+            pltpu.VMEM((2, experts, cols, rows), jnp.bfloat16),
+            pltpu.VMEM((2, experts, 1, cols), jnp.float32),
+            pltpu.VMEM((2, n, share, 1, cols), jnp.float32),
+            pltpu.VMEM((2, experts, 1, cols), jnp.float32),
+            pltpu.VMEM((ne, n, router_weight.shape[1], rows), jnp.bfloat16),
+            dma((SLOTS,)),
+            dma((2,)),
+            dma((2, n)),
+            dma((2, n)),
+            dma((2, n)),
+            dma((2, n)),
+            dma((2, n)),
+            dma((2, n)),
+            dma((n,)),
+            dma((n,)),
+            dma((ne,)),
+            dma((ne,)),
+        ],
+        compiler_params=pltpu.CompilerParams(
+            collective_id=0, has_side_effects=True, vmem_limit_bytes=60 * 2**20
+        ),
+        cost_estimate=pl.CostEstimate(
+            flops=4 * experts * rows * cols, bytes_accessed=20 * experts * rows * cols, transcendentals=0
+        ),
+    )(w_gate, w_up, router_weight.T, router_gain[None, :])
+    first = lax.axis_index("shard") * part
+    scale = lax.dynamic_slice_in_dim(scale[:, :, 0, :], first, part, axis=2)
+    return (jnp.swapaxes(gate, 1, 2), jnp.swapaxes(up, 1, 2), scale[0], scale[1], router)
+
+
 def solution(mesh):
     return jax.shard_map(
-        body,
+        functools.partial(body, mesh.shape["shard"], mesh.shape["expert"]),
         mesh=mesh,
         in_specs=(
             P("expert", "shard", None),

time: 774 us -> 589 us (0.76)
  Pallas kernels: 0 us -> 562 us
  blocking collectives: 299 us -> 0 us
  waiting for transfers between devices: 281 us -> 0 us
  local copies, waits for them, and re-layouts: 126 us -> 20 us
  other arithmetic: 41.5 us -> 0 us
  between operations: 14.1 us -> 0.65 us
  starting transfers between devices: 10.8 us -> 0 us
    pallas_call x0 -> x1, Pallas kernels: none -> 562 us  [body(): pl.pallas_call(functools.partial(kernel, n, ne, chunk), out_shape=(serve,...]
    all_gather x2 -> x0, blocking collectives: 299 us -> none  [the longest x1 292 us: body(): row_router = lax.all_gather(part_router, 'shard', axis=0, tiled=True)]
    all_to_all x2 -> x0, waiting for transfers between devices: 232 us -> none  [the longest x1 232 us: body(): lax.all_to_all(narrow_gate, 'shard', split_axis=2, concat_axis=1, tiled=T...]
    all_to_all x4 -> x0, local copies, waits for them, and re-layouts: 67.1 us -> none  [the longest x2 33.6 us: body(): lax.all_to_all(narrow_up, 'shard', split_axis=2, concat_axis=1, tiled=True)]
    pmax x1 -> x0, waiting for transfers between devices: 48.8 us -> none  [body(): lax.pmax((jnp.max(jnp.abs(w_gate), axis=1), jnp.max(jnp.abs(w_up), axis=1...]
    unnamed x11 -> x7, local copies, waits for them, and re-layouts: 56.4 us -> 18.5 us
    convert_element_type x3 -> x0, other arithmetic: 28.3 us -> none  [the longest x1 14.1 us: body(): (w_gate / jnp.expand_dims(scale_gate, 1)).astype(jnp.bfloat16)]
    reduce_max x2 -> x0, other arithmetic: 13.2 us -> none  [the longest x1 10.2 us: body(): jnp.max(jnp.abs(w_up), axis=1)]
  transfers between devices with their start and end apart: 3 -> 0, of which waited for: 2 -> 0; matrix products, arithmetic and copies ran while one was open for 10% -> 0% of each run, Pallas kernels for 0% -> 0%
where the time goes in v1:
time: 589 us; the launch traced here: 583 us
  Pallas kernels  562 us (95%)
  local copies, waits for them, and re-layouts  20 us (3%)
    pallas_call x1, Pallas kernels, body(): pl.pallas_call(functools.partial(kernel, n, ne, chunk), out_shape=(serve,...  562 us
    unnamed x7, local copies, waits for them, and re-layouts  18.5 us

profile of v1, /device:TPU:0, one launch (start us, length us, event | category | flops | bytes accessed | tf_op | source)
XLA Modules:
  0.0 583.0 jit_solution(2194291057275352176)
XLA Ops:
  0.6 562.3 %shard_map.83 = (bf16[32,96,2048]{2,1,0:T(8,128)(2,1)}, bf16[32,96,2048]{2,1,0:T(8,128)(2,1)}, f32[2,32,1,768]{3,2,1,0:T(1,128)}, bf16[2048,128]{1,0:T(8,128)(2,1)}) custom-call(f32[32,256,768]{2,1,0:T(8,128)} %gate.1, f32[32,256,768]{2,1,0:T(8,128)} %up.1, f32[32,256]{1,0:T(8,128)} %bitcast.8, f32[1,256]{1,0:T(1,128)} %bitcast.11), custom_call_target="tpu_custom_call" | custom-call | flops 25165824 | bytes 125829120 | tf_op jit(solution)/shard_map/pallas_call | solution.py:250
  563.0 1.5 constant_dynamic-slice_fusion.1
  564.5 0.0 copy-start
  564.5 11.4 %copy.12 = bf16[32,2048,96]{1,2,0:T(8,128)(2,1)} copy(bf16[32,2048,96]{1,2,0:T(8,128)(2,1)} %bitcast.7) | data formatting | bytes 25165824
  575.9 1.5 copy-done
  577.4 0.0 copy-start.1
  577.4 4.8 copy.13
  582.2 0.0 copy-done.1
  582.2 0.8 copy.14
Async XLA Ops:
  564.5 12.9 %copy-start = (bf16[32,96,2048]{2,1,0:T(8,128)(2,1)S(1)}, bf16[32,96,2048]{2,1,0:T(8,128)(2,1)}, u32[]{:S(2)}) copy-start(bf16[32,96,2048]{2,1,0:T(8,128)(2,1)} %get-tuple-element.10) | copy-start | bytes 37748740
  577.4 4.8 copy-start.1
